TPU v7x, 32 devices: a whole 2x2x4 slice. The times are simulated.
32 devices in a mesh: tm: 4 (over x, core), space: 8 (over z, y).
Axes of the slice: x: 2, y: 2, z: 4, core: 2. Of those that a mesh axis runs over, the one named last changes fastest.
Arguments:
- start_value: float32 [4, 8, 512, 256], P('tm', 'space'), may hold values from -6 to 6
- old_nodes: float32 [4, 3, 8, 512, 256], P('tm', None, 'space'), may hold values from -6 to 6
- diffusivity: float32 [8, 512, 256], P('space'), may hold values from 0.2 to 2
Outputs:
- fine_nodes: float32 [4, 3, 8, 512, 256], P('tm', None, 'space')
- next_start: float32 [4, 8, 512, 256], P('tm', 'space')
- next_coarse: float32 [4, 8, 512, 256], P('tm', 'space')
All inputs are finite; a program needn't handle non-finite values.
Results may differ from a plain program's by a relative error of at most 0.0001.
Values sent between devices are 32-bit elements; how exact they have to be, the bound alone decides.
A program may use at most 64 MiB of HBM per device.

v0:
```python
import math

import jax
import jax.numpy as jnp
from jax import lax
from jax.sharding import PartitionSpec as P

CG_ITERS = 2


STEP = 2.0
ROOT_SIX = math.sqrt(6.0)
NODE_TIMES = [(4.0 - ROOT_SIX) / 10.0, (4.0 + ROOT_SIX) / 10.0, 1.0]
COLLOC = [
    [
        (88.0 - 7.0 * ROOT_SIX) / 360.0,
        (296.0 - 169.0 * ROOT_SIX) / 1800.0,
        (-2.0 + 3.0 * ROOT_SIX) / 225.0,
    ],
    [
        (296.0 + 169.0 * ROOT_SIX) / 1800.0,
        (88.0 + 7.0 * ROOT_SIX) / 360.0,
        (-2.0 - 3.0 * ROOT_SIX) / 225.0,
    ],
    [(16.0 - ROOT_SIX) / 36.0, (16.0 + ROOT_SIX) / 36.0, 1.0 / 9.0],
]


def padded_2(value, sides, width):
    for axis, dim in sides:
        devices, length = (lax.axis_size(axis), value.shape[dim])
        up = [(i, (i + 1) % devices) for i in range(devices - 1)]
        down = [(j, i) for i, j in up]
        last = lax.slice_in_dim(value, length - width, length, axis=dim)
        leading = lax.slice_in_dim(value, 0, width, axis=dim)
        before = lax.ppermute(last, axis, up)
        after = lax.ppermute(leading, axis, down)
        value = jnp.concatenate([before, value, after], axis=dim)
    return value


def from_behind(block, axis, distance):
    devices = range(lax.axis_size(axis))
    route = [(i - distance, i) for i in devices if i - distance in devices]
    return lax.ppermute(block, axis, route)


def sweep_weight(row, column):
    below = COLLOC[row - 1][column] if row > 0 else 0.0
    return COLLOC[row][column] - below


def node_width(row):
    below = NODE_TIMES[row - 1] if row > 0 else 0.0
    return NODE_TIMES[row] - below


def neighbour(field, dim, forward):
    length = field.shape[dim]
    edge = jnp.zeros_like(lax.slice_in_dim(field, 0, 1, axis=dim))
    if forward:
        return jnp.concatenate([lax.slice_in_dim(field, 1, length, axis=dim), edge], axis=dim)
    return jnp.concatenate([edge, lax.slice_in_dim(field, 0, length - 1, axis=dim)], axis=dim)


def combine(weights, images):
    summed = weights[0] * images[0]
    for column in range(1, 3):
        summed = summed + weights[column] * images[column]
    return summed


def inner(left, right):
    return jnp.sum(left * right, axis=(1, 2, 3))


def widen(values):
    return values[:, None, None, None]


def paired(residual, image):
    return lax.psum((inner(residual, residual), inner(residual, image)), "space")


def solve(guess, residual, widths, heat):
    width_grid = widen(widths)
    iterate = guess
    image = residual - width_grid * heat(residual)
    norm_now, product_sum = paired(residual, image)
    step_size = norm_now / product_sum
    direction = residual
    along_image = image
    for sweep in range(CG_ITERS):
        iterate = iterate + widen(step_size) * direction
        if sweep + 1 < CG_ITERS:
            residual = residual - widen(step_size) * along_image
            image = residual - width_grid * heat(residual)
            norm_next, product_sum = paired(residual, image)
            momentum = norm_next / norm_now
            step_size = norm_next / (product_sum - momentum * norm_next / step_size)
            direction = residual + widen(momentum) * direction
            along_image = image + widen(momentum) * along_image
            norm_now = norm_next
    return iterate


def on_device(start_value, old_nodes, diffusivity):
    padded_kappa = padded_2(diffusivity, (("space", 0),), 1)
    kappa_after = padded_kappa[2:]
    kappa_before = padded_kappa[:-2]

    def heat(stacked):
        padded = padded_2(stacked, (("space", 1),), 1)
        face_one = 0.5 * (diffusivity + kappa_after)
        face_two = 0.5 * (diffusivity + kappa_before)
        face_three = 0.5 * (diffusivity + neighbour(diffusivity, 1, True))
        face_four = 0.5 * (diffusivity + neighbour(diffusivity, 1, False))
        face_five = 0.5 * (diffusivity + neighbour(diffusivity, 2, True))
        face_six = 0.5 * (diffusivity + neighbour(diffusivity, 2, False))
        total = face_one + face_two + face_three + face_four + face_five + face_six
        result = face_one * padded[:, 2:] + face_two * padded[:, :-2]
        result = (
            result
            + face_three * neighbour(stacked, 2, True)
            + face_four * neighbour(stacked, 2, False)
        )
        result = (
            result
            + face_five * neighbour(stacked, 3, True)
            + face_six * neighbour(stacked, 3, False)
        )
        return result - total * stacked

    previous_nodes = old_nodes[0]
    begin = start_value[0]
    images = heat(previous_nodes)

    def fine_residual(row, previous):
        weights = [sweep_weight(row, column) for column in range(3)]
        return previous - previous_nodes[row] + STEP * combine(weights, images)

    coarse_res = begin - previous_nodes[2] + STEP * combine(COLLOC[2], images)
    first_res = fine_residual(0, begin)
    fresh = [
        solve(
            previous_nodes[0:1],
            first_res[None],
            jnp.array([STEP * node_width(0)], jnp.float32),
            heat,
        )[0]
    ]
    coarse_end = None
    for row in range(1, 3):
        residual = fine_residual(row, fresh[row - 1])
        result = solve(
            previous_nodes[row : row + 1],
            residual[None],
            jnp.array([STEP * node_width(row)], jnp.float32),
            heat,
        )
        fresh.append(result[0])
    coarse_end = solve(previous_nodes[2:3], coarse_res[None], jnp.array([STEP], jnp.float32), heat)[
        0
    ]
    moved = from_behind(jnp.stack([fresh[2], coarse_end]), "tm", 1)
    first_slice = lax.axis_index("tm") == 0
    next_start = jnp.where(first_slice, begin, moved[0])[None]
    next_coarse = jnp.where(first_slice, begin, moved[1])[None]
    return (jnp.stack(fresh)[None], next_start, next_coarse)


def solution(mesh):
    in_specs = (
        P("tm", "space", None, None),
        P("tm", None, "space", None, None),
        P("space", None, None),
    )
    out_specs = (
        P("tm", None, "space", None, None),
        P("tm", "space", None, None),
        P("tm", "space", None, None),
    )
    return jax.shard_map(
        on_device, mesh=mesh, in_specs=in_specs, out_specs=out_specs, check_vma=False
    )
```

profile of v0, /device:TPU:1, one launch (start us, length us, event | category | flops | bytes accessed | tf_op | source)
XLA Modules:
  0.0 452.5 jit_solution(13187722062762523463)
XLA Ops:
  2.1 4.7 %collective-permute-start.3 = (f32[3,1,512,256]{3,2,1,0:T(8,128)}, f32[3,1,512,256]{3,2,1,0:T(8,128)S(1)}, u32[]{:S(2)}, u32[]{:S(2)}) collective-permute-start(f32[3,1,512,256]{3,2,1,0:T(8,128)} %bitcast.385), channel_id=1, source_target_pairs={{0,1},{1,2},{2,3},{3,4},{4,5},{5,6},{6,7},{8,9},{9,10},{10,11},{11... | collective-permute-start | bytes 4718600 | tf_op jit(solution)/shard_map/ppermute | solution.py:36
  8.1 4.8 %collective-permute-start.2 = (f32[1,512,256]{2,1,0:T(8,128)}, f32[1,512,256]{2,1,0:T(8,128)S(1)}, u32[]{:S(2)}, u32[]{:S(2)}) collective-permute-start(f32[1,512,256]{2,1,0:T(8,128)} %param.9), channel_id=1, source_target_pairs={{0,1},{1,2},{2,3},{3,4},{4,5},{5,6},{6,7},{8,9},{9,10},{10,11},{11... | collective-permute-start | bytes 1572872 | tf_op jit(solution)/shard_map/ppermute | solution.py:36
  16.0 34.3 %collective-permute-done = f32[1,512,256]{2,1,0:T(8,128)S(1)} collective-permute-done((f32[1,512,256]{2,1,0:T(8,128)}, f32[1,512,256]{2,1,0:T(8,128)S(1)}, u32[]{:S(2)}, u32[]{:S(2)}) %collective-permute-start) | collective-permute-done | bytes 524320 | tf_op jit(solution)/shard_map/ppermute | solution.py:37
  50.3 46.0 %collective-permute-done.2 = f32[1,512,256]{2,1,0:T(8,128)S(1)} collective-permute-done((f32[1,512,256]{2,1,0:T(8,128)}, f32[1,512,256]{2,1,0:T(8,128)S(1)}, u32[]{:S(2)}, u32[]{:S(2)}) %collective-permute-start.2) | collective-permute-done | bytes 524320 | tf_op jit(solution)/shard_map/ppermute | solution.py:36
  101.0 4.7 %collective-permute-start.5 = (f32[1,1,512,256]{3,2,1,0:T(8,128)S(1)}, f32[1,1,512,256]{3,2,1,0:T(8,128)S(1)}, u32[]{:S(2)}, u32[]{:S(2)}) collective-permute-start(f32[1,1,512,256]{3,2,1,0:T(8,128)S(1)} %get-tuple-element.51), channel_id=1, source_target_pairs={{0,1},{1,2},{2,3},{3,4},{4,5},{5,6},{6,7},{8,9},{9,10},{10,11},{11... | collective-permute-start | bytes 1572872 | tf_op jit(solution)/shard_map/ppermute | solution.py:36
  107.0 5.7 %collective-permute-start.17 = (f32[1,1,512,256]{3,2,1,0:T(8,128)}, f32[1,1,512,256]{3,2,1,0:T(8,128)}, u32[]{:S(2)}, u32[]{:S(2)}) collective-permute-start(f32[1,1,512,256]{3,2,1,0:T(8,128)} %get-tuple-element.50), channel_id=1, source_target_pairs={{0,1},{1,2},{2,3},{3,4},{4,5},{5,6},{6,7},{8,9},{9,10},{10,11},{11... | collective-permute-start | bytes 1572872 | tf_op jit(solution)/shard_map/ppermute | solution.py:36
  117.3 21.4 %collective-permute-done.5 = f32[1,1,512,256]{3,2,1,0:T(8,128)S(1)} collective-permute-done((f32[1,1,512,256]{3,2,1,0:T(8,128)S(1)}, f32[1,1,512,256]{3,2,1,0:T(8,128)S(1)}, u32[]{:S(2)}, u32[]{:S(2)}) %collective-permute-start.5) | collective-permute-done | bytes 524320 | tf_op jit(solution)/shard_map/ppermute | solution.py:36
  140.8 19.9 %all-reduce.45 = (f32[1]{0:T(128)}, f32[1]{0:T(128)}) all-reduce(f32[1]{0:T(128)} %bitcast.9, f32[1]{0:T(128)} %bitcast.17), channel_id=1, replica_groups=mesh['tm'=4,'space'=8] {'space'}, use_global_device_ids=true, to_apply=%region_1.0 | all-reduce | flops 2 | bytes 16 | tf_op jit(solution)/shard_map/psum | solution.py:82
  175.8 10.9 %collective-permute-done.7 = f32[1,1,512,256]{3,2,1,0:T(8,128)S(1)} collective-permute-done((f32[1,1,512,256]{3,2,1,0:T(8,128)S(1)}, f32[1,1,512,256]{3,2,1,0:T(8,128)S(1)}, u32[]{:S(2)}, u32[]{:S(2)}) %collective-permute-start.7) | collective-permute-done | bytes 524320 | tf_op jit(solution)/shard_map/ppermute | solution.py:36
  187.9 16.9 %all-reduce.44 = (f32[1]{0:T(128)}, f32[1]{0:T(128)}) all-reduce(f32[1]{0:T(128)} %bitcast.19, f32[1]{0:T(128)} %bitcast.20), channel_id=1, replica_groups=mesh['tm'=4,'space'=8] {'space'}, use_global_device_ids=true, to_apply=%region_5.0 | all-reduce | flops 2 | bytes 16 | tf_op jit(solution)/shard_map/psum | solution.py:82
  217.6 4.6 %collective-permute-done.8 = f32[1,1,512,256]{3,2,1,0:T(8,128)S(1)} collective-permute-done((f32[1,1,512,256]{3,2,1,0:T(8,128)S(1)}, f32[1,1,512,256]{3,2,1,0:T(8,128)S(1)}, u32[]{:S(2)}, u32[]{:S(2)}) %collective-permute-start.8) | collective-permute-done | bytes 524320 | tf_op jit(solution)/shard_map/ppermute | solution.py:37
  222.2 13.7 %collective-permute-done.9 = f32[1,1,512,256]{3,2,1,0:T(8,128)S(1)} collective-permute-done((f32[1,1,512,256]{3,2,1,0:T(8,128)S(1)}, f32[1,1,512,256]{3,2,1,0:T(8,128)S(1)}, u32[]{:S(2)}, u32[]{:S(2)}) %collective-permute-start.9) | collective-permute-done | bytes 524320 | tf_op jit(solution)/shard_map/ppermute | solution.py:36
  238.0 16.8 %all-reduce.43 = (f32[1]{0:T(128)}, f32[1]{0:T(128)}) all-reduce(f32[1]{0:T(128)} %bitcast.24, f32[1]{0:T(128)} %bitcast.25), channel_id=1, replica_groups=mesh['tm'=4,'space'=8] {'space'}, use_global_device_ids=true, to_apply=%region_9.0 | all-reduce | flops 2 | bytes 16 | tf_op jit(solution)/shard_map/psum | solution.py:82
  263.0 5.2 %collective-permute-done.10 = f32[1,1,512,256]{3,2,1,0:T(8,128)S(1)} collective-permute-done((f32[1,1,512,256]{3,2,1,0:T(8,128)S(1)}, f32[1,1,512,256]{3,2,1,0:T(8,128)S(1)}, u32[]{:S(2)}, u32[]{:S(2)}) %collective-permute-start.10) | collective-permute-done | bytes 524320 | tf_op jit(solution)/shard_map/ppermute | solution.py:37
  268.3 13.7 %collective-permute-done.11 = f32[1,1,512,256]{3,2,1,0:T(8,128)S(1)} collective-permute-done((f32[1,1,512,256]{3,2,1,0:T(8,128)S(1)}, f32[1,1,512,256]{3,2,1,0:T(8,128)S(1)}, u32[]{:S(2)}, u32[]{:S(2)}) %collective-permute-start.11) | collective-permute-done | bytes 524320 | tf_op jit(solution)/shard_map/ppermute | solution.py:36
  283.2 16.6 %all-reduce.42 = (f32[1]{0:T(128)}, f32[1]{0:T(128)}) all-reduce(f32[1]{0:T(128)} %bitcast.27, f32[1]{0:T(128)} %bitcast.28), channel_id=1, replica_groups=mesh['tm'=4,'space'=8] {'space'}, use_global_device_ids=true, to_apply=%region_13.0 | all-reduce | flops 2 | bytes 16 | tf_op jit(solution)/shard_map/psum | solution.py:82
  312.5 5.5 %collective-permute-done.12 = f32[1,1,512,256]{3,2,1,0:T(8,128)S(1)} collective-permute-done((f32[1,1,512,256]{3,2,1,0:T(8,128)S(1)}, f32[1,1,512,256]{3,2,1,0:T(8,128)S(1)}, u32[]{:S(2)}, u32[]{:S(2)}) %collective-permute-start.12) | collective-permute-done | bytes 524320 | tf_op jit(solution)/shard_map/ppermute | solution.py:37
  318.0 13.8 %collective-permute-done.13 = f32[1,1,512,256]{3,2,1,0:T(8,128)S(1)} collective-permute-done((f32[1,1,512,256]{3,2,1,0:T(8,128)S(1)}, f32[1,1,512,256]{3,2,1,0:T(8,128)S(1)}, u32[]{:S(2)}, u32[]{:S(2)}) %collective-permute-start.13) | collective-permute-done | bytes 524320 | tf_op jit(solution)/shard_map/ppermute | solution.py:36
  333.8 16.6 %all-reduce.41 = (f32[1]{0:T(128)}, f32[1]{0:T(128)}, f32[1]{0:T(128)}, f32[1]{0:T(128)}) all-reduce(f32[1]{0:T(128)} %bitcast.32, f32[1]{0:T(128)} %bitcast.33, f32[1]{0:T(128)} %bitcast.40, f32[1]{0:T(128)} %bitcast.41), channel_id=1, replica_groups=mesh['tm'=4,'space'=8] {'space'}, use_global_device_ids=true, to_apply=%region_17.0 | all-reduce | flops 4 | bytes 32 | tf_op jit(solution)/shard_map/psum | solution.py:82
  366.2 25.0 %collective-permute-done.19 = f32[1,1,512,256]{3,2,1,0:T(8,128)S(1)} collective-permute-done((f32[1,1,512,256]{3,2,1,0:T(8,128)S(1)}, f32[1,1,512,256]{3,2,1,0:T(8,128)S(1)}, u32[]{:S(2)}, u32[]{:S(2)}) %collective-permute-start.19) | collective-permute-done | bytes 524320 | tf_op jit(solution)/shard_map/ppermute | solution.py:36
  392.4 10.0 %collective-permute-done.15 = f32[1,1,512,256]{3,2,1,0:T(8,128)S(1)} collective-permute-done((f32[1,1,512,256]{3,2,1,0:T(8,128)S(1)}, f32[1,1,512,256]{3,2,1,0:T(8,128)S(1)}, u32[]{:S(2)}, u32[]{:S(2)}) %collective-permute-start.15) | collective-permute-done | bytes 524320 | tf_op jit(solution)/shard_map/ppermute | solution.py:36
  403.5 16.6 %all-reduce.40 = (f32[1]{0:T(128)}, f32[1]{0:T(128)}, f32[1]{0:T(128)}, f32[1]{0:T(128)}) all-reduce(f32[1]{0:T(128)} %bitcast.35, f32[1]{0:T(128)} %bitcast.36, f32[1]{0:T(128)} %bitcast.43, f32[1]{0:T(128)} %bitcast.44), channel_id=1, replica_groups=mesh['tm'=4,'space'=8] {'space'}, use_global_device_ids=true, to_apply=%region_21.0 | all-reduce | flops 4 | bytes 32 | tf_op jit(solution)/shard_map/psum | solution.py:82
  432.2 7.2 %collective-permute-start.20 = (f32[2,1,512,256]{3,2,1,0:T(8,128)}, f32[2,1,512,256]{3,2,1,0:T(8,128)S(1)}, u32[]{:S(2)}, u32[]{:S(2)}) collective-permute-start(f32[2,1,512,256]{3,2,1,0:T(8,128)} %pad_maximum_fusion), channel_id=1, source_target_pairs={{0,8},{8,16},{16,24},{1,9},{9,17},{17,25},{2,10},{10,18},{18,26},{... | collective-permute-start | bytes 3145736 | tf_op jit(solution)/shard_map/ppermute | solution.py:45
  440.7 10.8 %collective-permute-done.20 = f32[2,1,512,256]{3,2,1,0:T(8,128)S(1)} collective-permute-done((f32[2,1,512,256]{3,2,1,0:T(8,128)}, f32[2,1,512,256]{3,2,1,0:T(8,128)S(1)}, u32[]{:S(2)}, u32[]{:S(2)}) %collective-permute-start.20) | collective-permute-done | bytes 1048608 | tf_op jit(solution)/shard_map/ppermute | solution.py:45
  (136 shorter events, 82.6 us)
Async XLA Ops:
  0.6 96.0 %collective-permute-start.1 = (f32[3,1,512,256]{3,2,1,0:T(8,128)}, f32[3,1,512,256]{3,2,1,0:T(8,128)S(1)}, u32[]{:S(2)}, u32[]{:S(2)}) collective-permute-start(f32[3,1,512,256]{3,2,1,0:T(8,128)} %bitcast.384), channel_id=1, source_target_pairs={{1,0},{2,1},{3,2},{4,3},{5,4},{6,5},{7,6},{9,8},{10,9},{11,10},{12... | collective-permute-start | bytes 4718600 | tf_op jit(solution)/shard_map/ppermute | solution.py:37
  2.1 94.6 %collective-permute-start.3 = (f32[3,1,512,256]{3,2,1,0:T(8,128)}, f32[3,1,512,256]{3,2,1,0:T(8,128)S(1)}, u32[]{:S(2)}, u32[]{:S(2)}) collective-permute-start(f32[3,1,512,256]{3,2,1,0:T(8,128)} %bitcast.385), channel_id=1, source_target_pairs={{0,1},{1,2},{2,3},{3,4},{4,5},{5,6},{6,7},{8,9},{9,10},{10,11},{11... | collective-permute-start | bytes 4718600 | tf_op jit(solution)/shard_map/ppermute | solution.py:36
  6.8 43.5 %collective-permute-start = (f32[1,512,256]{2,1,0:T(8,128)}, f32[1,512,256]{2,1,0:T(8,128)S(1)}, u32[]{:S(2)}, u32[]{:S(2)}) collective-permute-start(f32[1,512,256]{2,1,0:T(8,128)} %param.9), channel_id=1, source_target_pairs={{1,0},{2,1},{3,2},{4,3},{5,4},{6,5},{7,6},{9,8},{10,9},{11,10},{12... | collective-permute-start | bytes 1572872 | tf_op jit(solution)/shard_map/ppermute | solution.py:37
  8.1 88.2 %collective-permute-start.2 = (f32[1,512,256]{2,1,0:T(8,128)}, f32[1,512,256]{2,1,0:T(8,128)S(1)}, u32[]{:S(2)}, u32[]{:S(2)}) collective-permute-start(f32[1,512,256]{2,1,0:T(8,128)} %param.9), channel_id=1, source_target_pairs={{0,1},{1,2},{2,3},{3,4},{4,5},{5,6},{6,7},{8,9},{9,10},{10,11},{11... | collective-permute-start | bytes 1572872 | tf_op jit(solution)/shard_map/ppermute | solution.py:36
  96.6 42.1 %copy-start.1 = (f32[1,512,256]{2,1,0:T(8,128)}, f32[1,512,256]{2,1,0:T(8,128)S(1)}, u32[]{:S(2)}) copy-start(f32[1,512,256]{2,1,0:T(8,128)S(1)} %get-tuple-element.47) | copy-start | bytes 1572868
  96.6 42.1 %copy-start.7 = (f32[1,512,256]{2,1,0:T(8,128)}, f32[1,512,256]{2,1,0:T(8,128)S(1)}, u32[]{:S(2)}) copy-start(f32[1,512,256]{2,1,0:T(8,128)S(1)} %get-tuple-element.48) | copy-start | bytes 1572868
  99.7 17.6 %collective-permute-start.4 = (f32[1,1,512,256]{3,2,1,0:T(8,128)S(1)}, f32[1,1,512,256]{3,2,1,0:T(8,128)S(1)}, u32[]{:S(2)}, u32[]{:S(2)}) collective-permute-start(f32[1,1,512,256]{3,2,1,0:T(8,128)S(1)} %get-tuple-element.51), channel_id=1, source_target_pairs={{1,0},{2,1},{3,2},{4,3},{5,4},{6,5},{7,6},{9,8},{10,9},{11,10},{12... | collective-permute-start | bytes 1572872 | tf_op jit(solution)/shard_map/ppermute | solution.py:37
  101.0 37.7 %collective-permute-start.5 = (f32[1,1,512,256]{3,2,1,0:T(8,128)S(1)}, f32[1,1,512,256]{3,2,1,0:T(8,128)S(1)}, u32[]{:S(2)}, u32[]{:S(2)}) collective-permute-start(f32[1,1,512,256]{3,2,1,0:T(8,128)S(1)} %get-tuple-element.51), channel_id=1, source_target_pairs={{0,1},{1,2},{2,3},{3,4},{4,5},{5,6},{6,7},{8,9},{9,10},{10,11},{11... | collective-permute-start | bytes 1572872 | tf_op jit(solution)/shard_map/ppermute | solution.py:36
  105.7 63.3 %collective-permute-start.16 = (f32[1,1,512,256]{3,2,1,0:T(8,128)}, f32[1,1,512,256]{3,2,1,0:T(8,128)}, u32[]{:S(2)}, u32[]{:S(2)}) collective-permute-start(f32[1,1,512,256]{3,2,1,0:T(8,128)} %get-tuple-element.50), channel_id=1, source_target_pairs={{1,0},{2,1},{3,2},{4,3},{5,4},{6,5},{7,6},{9,8},{10,9},{11,10},{12... | collective-permute-start | bytes 1572872 | tf_op jit(solution)/shard_map/ppermute | solution.py:37
  107.0 62.0 %collective-permute-start.17 = (f32[1,1,512,256]{3,2,1,0:T(8,128)}, f32[1,1,512,256]{3,2,1,0:T(8,128)}, u32[]{:S(2)}, u32[]{:S(2)}) collective-permute-start(f32[1,1,512,256]{3,2,1,0:T(8,128)} %get-tuple-element.50), channel_id=1, source_target_pairs={{0,1},{1,2},{2,3},{3,4},{4,5},{5,6},{6,7},{8,9},{9,10},{10,11},{11... | collective-permute-start | bytes 1572872 | tf_op jit(solution)/shard_map/ppermute | solution.py:36
  163.3 12.6 %collective-permute-start.6 = (f32[1,1,512,256]{3,2,1,0:T(8,128)S(1)}, f32[1,1,512,256]{3,2,1,0:T(8,128)S(1)}, u32[]{:S(2)}, u32[]{:S(2)}) collective-permute-start(f32[1,1,512,256]{3,2,1,0:T(8,128)S(1)} %multiply_subtract_fusion.4), channel_id=1, source_target_pairs={{1,0},{2,1},{3,2},{4,3},{5,4},{6,5},{7,6},{9,8},{10,9},{11,10},{12... | collective-permute-start | bytes 1572872 | tf_op jit(solution)/shard_map/ppermute | solution.py:37
  164.6 22.1 %collective-permute-start.7 = (f32[1,1,512,256]{3,2,1,0:T(8,128)S(1)}, f32[1,1,512,256]{3,2,1,0:T(8,128)S(1)}, u32[]{:S(2)}, u32[]{:S(2)}) collective-permute-start(f32[1,1,512,256]{3,2,1,0:T(8,128)S(1)} %multiply_subtract_fusion.4), channel_id=1, source_target_pairs={{0,1},{1,2},{2,3},{3,4},{4,5},{5,6},{6,7},{8,9},{9,10},{10,11},{11... | collective-permute-start | bytes 1572872 | tf_op jit(solution)/shard_map/ppermute | solution.py:36
  212.0 10.3 %collective-permute-start.8 = (f32[1,1,512,256]{3,2,1,0:T(8,128)S(1)}, f32[1,1,512,256]{3,2,1,0:T(8,128)S(1)}, u32[]{:S(2)}, u32[]{:S(2)}) collective-permute-start(f32[1,1,512,256]{3,2,1,0:T(8,128)S(1)} %get-tuple-element.40), channel_id=1, source_target_pairs={{1,0},{2,1},{3,2},{4,3},{5,4},{6,5},{7,6},{9,8},{10,9},{11,10},{12... | collective-permute-start | bytes 1572872 | tf_op jit(solution)/shard_map/ppermute | solution.py:37
  213.2 22.7 %collective-permute-start.9 = (f32[1,1,512,256]{3,2,1,0:T(8,128)S(1)}, f32[1,1,512,256]{3,2,1,0:T(8,128)S(1)}, u32[]{:S(2)}, u32[]{:S(2)}) collective-permute-start(f32[1,1,512,256]{3,2,1,0:T(8,128)S(1)} %get-tuple-element.40), channel_id=1, source_target_pairs={{0,1},{1,2},{2,3},{3,4},{4,5},{5,6},{6,7},{8,9},{9,10},{10,11},{11... | collective-permute-start | bytes 1572872 | tf_op jit(solution)/shard_map/ppermute | solution.py:36
  257.4 10.9 %collective-permute-start.10 = (f32[1,1,512,256]{3,2,1,0:T(8,128)S(1)}, f32[1,1,512,256]{3,2,1,0:T(8,128)S(1)}, u32[]{:S(2)}, u32[]{:S(2)}) collective-permute-start(f32[1,1,512,256]{3,2,1,0:T(8,128)S(1)} %multiply_subtract_fusion.3), channel_id=1, source_target_pairs={{1,0},{2,1},{3,2},{4,3},{5,4},{6,5},{7,6},{9,8},{10,9},{11,10},{12... | collective-permute-start | bytes 1572872 | tf_op jit(solution)/shard_map/ppermute | solution.py:37
  258.7 23.3 %collective-permute-start.11 = (f32[1,1,512,256]{3,2,1,0:T(8,128)S(1)}, f32[1,1,512,256]{3,2,1,0:T(8,128)S(1)}, u32[]{:S(2)}, u32[]{:S(2)}) collective-permute-start(f32[1,1,512,256]{3,2,1,0:T(8,128)S(1)} %multiply_subtract_fusion.3), channel_id=1, source_target_pairs={{0,1},{1,2},{2,3},{3,4},{4,5},{5,6},{6,7},{8,9},{9,10},{10,11},{11... | collective-permute-start | bytes 1572872 | tf_op jit(solution)/shard_map/ppermute | solution.py:36
  306.9 11.2 %collective-permute-start.12 = (f32[1,1,512,256]{3,2,1,0:T(8,128)S(1)}, f32[1,1,512,256]{3,2,1,0:T(8,128)S(1)}, u32[]{:S(2)}, u32[]{:S(2)}) collective-permute-start(f32[1,1,512,256]{3,2,1,0:T(8,128)S(1)} %get-tuple-element.37), channel_id=1, source_target_pairs={{1,0},{2,1},{3,2},{4,3},{5,4},{6,5},{7,6},{9,8},{10,9},{11,10},{12... | collective-permute-start | bytes 1572872 | tf_op jit(solution)/shard_map/ppermute | solution.py:37
  308.2 23.6 %collective-permute-start.13 = (f32[1,1,512,256]{3,2,1,0:T(8,128)S(1)}, f32[1,1,512,256]{3,2,1,0:T(8,128)S(1)}, u32[]{:S(2)}, u32[]{:S(2)}) collective-permute-start(f32[1,1,512,256]{3,2,1,0:T(8,128)S(1)} %get-tuple-element.37), channel_id=1, source_target_pairs={{0,1},{1,2},{2,3},{3,4},{4,5},{5,6},{6,7},{8,9},{9,10},{10,11},{11... | collective-permute-start | bytes 1572872 | tf_op jit(solution)/shard_map/ppermute | solution.py:36
  354.7 47.7 %copy-start.23 = (f32[1,1,512,256]{3,2,1,0:T(8,128)}, f32[1,1,512,256]{3,2,1,0:T(8,128)S(1)}, u32[]{:S(2)}) copy-start(f32[1,1,512,256]{3,2,1,0:T(8,128)S(1)} %get-tuple-element.97) | copy-start | bytes 1572868
  355.0 11.2 %collective-permute-start.18 = (f32[1,1,512,256]{3,2,1,0:T(8,128)S(1)}, f32[1,1,512,256]{3,2,1,0:T(8,128)S(1)}, u32[]{:S(2)}, u32[]{:S(2)}) collective-permute-start(f32[1,1,512,256]{3,2,1,0:T(8,128)S(1)} %get-tuple-element.96), channel_id=1, source_target_pairs={{1,0},{2,1},{3,2},{4,3},{5,4},{6,5},{7,6},{9,8},{10,9},{11,10},{12... | collective-permute-start | bytes 1572872 | tf_op jit(solution)/shard_map/ppermute | solution.py:37
  356.3 34.9 %collective-permute-start.19 = (f32[1,1,512,256]{3,2,1,0:T(8,128)S(1)}, f32[1,1,512,256]{3,2,1,0:T(8,128)S(1)}, u32[]{:S(2)}, u32[]{:S(2)}) collective-permute-start(f32[1,1,512,256]{3,2,1,0:T(8,128)S(1)} %get-tuple-element.96), channel_id=1, source_target_pairs={{0,1},{1,2},{2,3},{3,4},{4,5},{5,6},{6,7},{8,9},{9,10},{10,11},{11... | collective-permute-start | bytes 1572872 | tf_op jit(solution)/shard_map/ppermute | solution.py:36
  360.5 31.9 %collective-permute-start.14 = (f32[1,1,512,256]{3,2,1,0:T(8,128)S(1)}, f32[1,1,512,256]{3,2,1,0:T(8,128)S(1)}, u32[]{:S(2)}, u32[]{:S(2)}) collective-permute-start(f32[1,1,512,256]{3,2,1,0:T(8,128)S(1)} %get-tuple-element.97), channel_id=1, source_target_pairs={{1,0},{2,1},{3,2},{4,3},{5,4},{6,5},{7,6},{9,8},{10,9},{11,10},{12... | collective-permute-start | bytes 1572872 | tf_op jit(solution)/shard_map/ppermute | solution.py:37
  361.8 40.6 %collective-permute-start.15 = (f32[1,1,512,256]{3,2,1,0:T(8,128)S(1)}, f32[1,1,512,256]{3,2,1,0:T(8,128)S(1)}, u32[]{:S(2)}, u32[]{:S(2)}) collective-permute-start(f32[1,1,512,256]{3,2,1,0:T(8,128)S(1)} %get-tuple-element.97), channel_id=1, source_target_pairs={{0,1},{1,2},{2,3},{3,4},{4,5},{5,6},{6,7},{8,9},{9,10},{10,11},{11... | collective-permute-start | bytes 1572872 | tf_op jit(solution)/shard_map/ppermute | solution.py:36
  432.2 19.2 %collective-permute-start.20 = (f32[2,1,512,256]{3,2,1,0:T(8,128)}, f32[2,1,512,256]{3,2,1,0:T(8,128)S(1)}, u32[]{:S(2)}, u32[]{:S(2)}) collective-permute-start(f32[2,1,512,256]{3,2,1,0:T(8,128)} %pad_maximum_fusion), channel_id=1, source_target_pairs={{0,8},{8,16},{16,24},{1,9},{9,17},{17,25},{2,10},{10,18},{18,26},{... | collective-permute-start | bytes 3145736 | tf_op jit(solution)/shard_map/ppermute | solution.py:45
  (33 other events, 518.8 us)
where the time goes:
time: 454 us; the launch traced here: 452 us
  waiting for transfers between devices  217 us (48%)
  blocking collectives  103 us (23%)
  starting transfers between devices  64.4 us (14%)
  other arithmetic  31.9 us (7%)
  between operations  24.4 us (5%)
  local copies, waits for them, and re-layouts  11.5 us (3%)
    ppermute x10, waiting for transfers between devices, padded_2(): before = lax.ppermute(last, axis, up)  154 us
    psum x6, blocking collectives, paired(): lax.psum((inner(residual, residual), inner(residual, image)), 'space')  103 us
    ppermute x10, waiting for transfers between devices, padded_2(): after = lax.ppermute(leading, axis, down)  51.6 us
    ppermute x10, starting transfers between devices, padded_2(): before = lax.ppermute(last, axis, up)  44.1 us
    reduce_sum x8, other arithmetic, inner(): return jnp.sum(left * right, axis=(1, 2, 3))  14.1 us
    ppermute x10, starting transfers between devices, padded_2(): after = lax.ppermute(leading, axis, down)  13 us
    ppermute x1, waiting for transfers between devices, from_behind(): return lax.ppermute(block, axis, route)  10.8 us
  transfers between devices with their start and end apart: 21, of which 14 were waited for; matrix products, arithmetic and copies ran while one was open for 4% of the time, Pallas kernels for 0%

commit v1 on v0

v1 whole, which is shorter than its diff:
```python
import math

import jax
import jax.numpy as jnp
from jax import lax
from jax.experimental import pallas as pl
from jax.experimental.pallas import tpu as pltpu
from jax.sharding import PartitionSpec as P

STEP = 2.0
ROOT_SIX = math.sqrt(6.0)
NODE_TIMES = [(4.0 - ROOT_SIX) / 10.0, (4.0 + ROOT_SIX) / 10.0, 1.0]
COLLOC = [
    [
        (88.0 - 7.0 * ROOT_SIX) / 360.0,
        (296.0 - 169.0 * ROOT_SIX) / 1800.0,
        (-2.0 + 3.0 * ROOT_SIX) / 225.0,
    ],
    [
        (296.0 + 169.0 * ROOT_SIX) / 1800.0,
        (88.0 + 7.0 * ROOT_SIX) / 360.0,
        (-2.0 - 3.0 * ROOT_SIX) / 225.0,
    ],
    [(16.0 - ROOT_SIX) / 36.0, (16.0 + ROOT_SIX) / 36.0, 1.0 / 9.0],
]
MESH = pl.DeviceIdType.MESH
PAD = 8

KAPPA, NODE, START, RES, IMG = 0, 1, 4, 5, 9
FIELDS = 13
H_KAPPA, H_NODE, H_RES, H_IMG = 0, 1, 4, 8
HALOS = 12


def sweep_weight(row, column):
    below = COLLOC[row - 1][column] if row > 0 else 0.0
    return COLLOC[row][column] - below


def node_width(row):
    below = NODE_TIMES[row - 1] if row > 0 else 0.0
    return NODE_TIMES[row] - below


WIDTHS = [STEP * node_width(0), STEP * node_width(1), STEP * node_width(2), STEP]


def tile_of(rows, most):
    best = 8
    for size in range(8, most + 1, 8):
        if rows % size == 0:
            best = size
    return best


def kernel(
    slices, slabs, ny, nz,
    start_in, nodes_in, kappa_in,
    fine_out, start_out, coarse_out,
    field, lower, upper, faces, across, image, base, result, staged, mail, sums,
    swap_s, swap_r, own_s, halo_s, halo_r, sum_s, sum_r, out_s, out_r, keep_s, end_s, end_r, copy_s,
):
    f32 = jnp.float32
    t = lax.axis_index("tm")
    s = lax.axis_index("space")
    h = lax.rem(s, 2)
    p = lax.div(s, 2)
    pairs = slabs // 2
    half = ny // 2
    win = half + PAD
    other = 1 - h
    partner = s + 1 - 2 * h
    first_row = pl.multiple_of(h * (half - PAD), 8)
    partner_row = pl.multiple_of(other * (half - PAD), 8)
    own = pl.multiple_of(PAD * h, 8)
    mine = pl.multiple_of(h * half, 8)
    has_next = t < slices - 1
    has_prev = t > 0
    has_lower = p > 0
    has_upper = p < pairs - 1
    pending = []

    def start(copy, cond=None):
        if cond is None:
            copy.start()
        else:
            pl.when(cond)(copy.start)
        return copy

    def later(copy, cond=None):
        pending.append((copy, cond))

    def remote(src, dst, send, recv, tm, space):
        return pltpu.make_async_remote_copy(
            src_ref=src, dst_ref=dst, send_sem=send, recv_sem=recv,
            device_id=(tm, space), device_id_type=MESH,
        )

    barrier = pltpu.get_barrier_semaphore()

    def greet(d, carry):
        pl.semaphore_signal(
            barrier, inc=1, device_id=(t, lax.rem(s + d, slabs)), device_id_type=MESH
        )
        return carry

    lax.fori_loop(1, slabs, greet, 0)
    for cond, tm in ((has_next, t + 1), (has_prev, t - 1)):

        @pl.when(cond)
        def _(tm=tm):
            for space in (s, partner):
                pl.semaphore_signal(barrier, inc=1, device_id=(tm, space), device_id_type=MESH)

    sources = [kappa_in.at[0]] + [nodes_in.at[0, j, 0] for j in range(3)] + [start_in.at[0, 0]]
    loads = []
    for k, source in enumerate(sources):
        loads.append(
            start(
                pltpu.make_async_copy(
                    source.at[pl.ds(first_row, win)], field.at[k, h, pl.ds(PAD, win)], own_s.at[k]
                )
            )
        )

    zeros = jnp.zeros((PAD, nz), f32)
    for k in range(FIELDS):
        for slab in range(2):
            field[k, slab, 0:PAD, :] = zeros
            field[k, slab, win + PAD : win + 2 * PAD, :] = zeros

    def clear(ref):
        def body(i, carry):
            for k in range(HALOS):
                ref[k, pl.ds(pl.multiple_of(i * 8, 8), 8), :] = zeros
            return carry

        lax.fori_loop(0, win // 8, body, 0)

    @pl.when(jnp.logical_not(has_lower))
    def _():
        clear(lower)

    @pl.when(jnp.logical_not(has_upper))
    def _():
        clear(upper)

    pl.semaphore_wait(
        barrier,
        slabs - 1 + 2 * has_next.astype(jnp.int32) + 2 * has_prev.astype(jnp.int32),
    )

    chunk = tile_of(win, win // 3)
    chunks = win // chunk

    def swap_copy(k, c):
        return remote(
            sources[k].at[pl.ds(partner_row + c * chunk, chunk)],
            field.at[k, h, pl.ds(PAD + c * chunk, chunk)],
            swap_s.at[k, c], swap_r.at[k, c], t, partner,
        )

    def swap_wait(k, c):
        remote(
            field.at[k, other, pl.ds(PAD + c * chunk, chunk)],
            field.at[k, other, pl.ds(PAD + c * chunk, chunk)],
            swap_s.at[k, c], swap_r.at[k, c], t, partner,
        ).wait_recv()

    for k in range(5):
        for c in range(chunks):
            later(start(swap_copy(k, c)))

    def down(f, k, c, lo, rows):
        return remote(
            field.at[f, 0, pl.ds(PAD + lo, rows)], upper.at[k, pl.ds(lo, rows)],
            halo_s.at[k, 0, c], halo_r.at[k, 0, c], t, s - 2,
        )

    def up(f, k, c, lo, rows):
        return remote(
            field.at[f, 1, pl.ds(PAD + lo, rows)], lower.at[k, pl.ds(lo, rows)],
            halo_s.at[k, 1, c], halo_r.at[k, 1, c], t, s + 2,
        )

    def first_hop(k, c, which):
        @pl.when(jnp.logical_and(which == 0, has_lower))
        def _():
            down(k, k, c, c * chunk, chunk).start()

        @pl.when(jnp.logical_and(which == 1, has_upper))
        def _():
            up(k, k, c, c * chunk, chunk).start()

    for k in range(4):
        loads[k].wait()
        for c in range(chunks):
            first_hop(k, c, h)
    loads[4].wait()

    def pass_on(k):
        for c in range(chunks):
            swap_wait(k, c)
            first_hop(k, c, other)

    def halo_wait(k, c, lo, rows, sides=(0, 1)):
        if 0 in sides:

            @pl.when(has_upper)
            def _():
                remote(
                    upper.at[k, pl.ds(lo, rows)], upper.at[k, pl.ds(lo, rows)],
                    halo_s.at[k, 0, c], halo_r.at[k, 0, c], t, s + 2,
                ).wait_recv()

        if 1 in sides:

            @pl.when(has_lower)
            def _():
                remote(
                    lower.at[k, pl.ds(lo, rows)], lower.at[k, pl.ds(lo, rows)],
                    halo_s.at[k, 1, c], halo_r.at[k, 1, c], t, s - 2,
                ).wait_recv()

    def halo_sent(f, k, c, lo, rows):
        later(down(f, k, c, lo, rows), has_lower)
        later(up(f, k, c, lo, rows), has_upper)

    for k in range(4):
        for c in range(chunks):
            halo_sent(k, k, c, c * chunk, chunk)

    tile = tile_of(win, 24)
    lane = lax.broadcasted_iota(jnp.int32, (tile, nz), 1)

    def loop(rows, size, body, init=0, offset=0):
        def step(i, carry):
            return body(pl.multiple_of(offset + i * size, 8), carry)

        return lax.fori_loop(0, rows // size, step, init)

    def coefficients(b, carry):
        windows = [field[KAPPA, slab, pl.ds(b, tile + 2 * PAD), :] for slab in range(2)]
        centre = [w[PAD : PAD + tile] for w in windows]
        before = 0.5 * (centre[0] + lower[H_KAPPA, pl.ds(b, tile), :])
        between = 0.5 * (centre[0] + centre[1])
        after = 0.5 * (centre[1] + upper[H_KAPPA, pl.ds(b, tile), :])
        across[0, pl.ds(b, tile), :] = before
        across[1, pl.ds(b, tile), :] = between
        across[2, pl.ds(b, tile), :] = after
        ends = [before + between, between + after]
        for slab in range(2):
            w, k = windows[slab], centre[slab]
            above = 0.5 * (k + w[PAD - 1 : PAD - 1 + tile])
            below = 0.5 * (k + w[PAD + 1 : PAD + 1 + tile])
            right = jnp.where(lane == nz - 1, 0.0, pltpu.roll(k, nz - 1, axis=1))
            left = jnp.where(lane == 0, 0.0, pltpu.roll(k, 1, axis=1))
            right_face = 0.5 * (k + right)
            left_face = 0.5 * (k + left)
            faces[0, slab, pl.ds(b, tile), :] = above
            faces[1, slab, pl.ds(b, tile), :] = below
            faces[2, slab, pl.ds(b, tile), :] = jnp.where(lane == nz - 1, 0.0, right_face)
            faces[3, slab, pl.ds(b, tile), :] = ends[slab] + above + below + right_face + left_face
        return carry

    def heat(windows, outer, b, size):
        centre = [w[PAD : PAD + size] for w in windows]
        between = across[1, pl.ds(b, size), :]
        images = []
        for slab in range(2):
            w, v = windows[slab], centre[slab]
            fz = faces[2, slab, pl.ds(b, size), :]
            value = between * centre[1 - slab]
            if outer[slab] is not None:
                value = value + outer[slab]
            value = value + faces[0, slab, pl.ds(b, size), :] * w[PAD - 1 : PAD - 1 + size]
            value = value + faces[1, slab, pl.ds(b, size), :] * w[PAD + 1 : PAD + 1 + size]
            value = value + fz * pltpu.roll(v, nz - 1, axis=1) + pltpu.roll(fz * v, 1, axis=1)
            images.append(value - faces[3, slab, pl.ds(b, size), :] * v)
        return centre, images

    def plain_heat(f, k, b, size):
        windows = [field[f, slab, pl.ds(b, size + 2 * PAD), :] for slab in range(2)]
        outer = (
            across[0, pl.ds(b, size), :] * lower[k, pl.ds(b, size), :],
            across[2, pl.ds(b, size), :] * upper[k, pl.ds(b, size), :],
        )
        return heat(windows, outer, b, size)

    def folded(value):
        return jnp.sum(value.reshape(-1, 8, nz), axis=0)

    def sum_copy(e, d):
        return remote(
            sums.at[e, s], sums.at[e, s], sum_s.at[e, d], sum_r.at[e, d],
            t, lax.rem(s + d, slabs),
        )

    def sum_start(e, parts):
        for row, part in enumerate(parts):
            flat = jnp.sum(part, axis=0, keepdims=True)
            line = flat[:, 0:128]
            for at in range(128, nz, 128):
                line = line + flat[:, at : at + 128]
            sums[e, s, row : row + 1, :] = line

        def body(d, carry):
            sum_copy(e, d).start()
            return carry

        lax.fori_loop(1, slabs, body, 0)

    def sum_wait(e):
        def body(d, carry):
            source = lax.rem(s - d + slabs, slabs)
            remote(
                sums.at[e, source], sums.at[e, source], sum_s.at[e, d], sum_r.at[e, d],
                t, source,
            ).wait_recv()
            return carry

        lax.fori_loop(1, slabs, body, 0)
        total = jnp.sum(sums[e], axis=0)
        total = jnp.sum(total, axis=1, keepdims=True)
        return total[0:1, :], total[1:2, :]

    def res_send(m):
        start(down(RES + m, H_RES + m, 0, 0, win), has_lower)
        start(up(RES + m, H_RES + m, 0, 0, win), has_upper)
        halo_sent(RES + m, H_RES + m, 0, 0, win)

    quarter = half // 2
    set_up = own
    set_down = pl.multiple_of(own + quarter, 8)

    def img_send(m):
        copies = (
            (down(IMG + m, H_IMG + m, 0, set_down, quarter), has_lower),
            (up(IMG + m, H_IMG + m, 0, set_up, quarter), has_upper),
        )
        for copy, cond in copies:
            start(copy, cond)
            later(copy, cond)

    def product(m):
        halo_wait(H_RES + m, 0, 0, win)

        def body(b, carry):
            centre, images = plain_heat(RES + m, H_RES + m, b, tile)
            row = lax.broadcasted_iota(jnp.int32, (tile, nz), 0) + b
            inside = jnp.logical_and(row >= own, row < own + half)
            norm, along = carry
            for slab in range(2):
                v = centre[slab]
                z = v - WIDTHS[m] * images[slab]
                field[IMG + m, slab, pl.ds(PAD + b, tile), :] = z
                masked = jnp.where(inside, v, 0.0)
                norm = norm + folded(masked * v)
                along = along + folded(masked * z)
            return norm, along

        nothing = jnp.zeros((8, nz), f32)
        norm, along = loop(win, tile, body, (nothing, nothing))
        img_send(m)
        sum_start(2 * m, (norm, along))

    small = tile_of(quarter, 32)

    def second(m):
        norm_now, along = sum_wait(2 * m)
        step_size = norm_now / along
        halo_wait(H_IMG + m, 0, set_down, quarter, (0,))
        halo_wait(H_IMG + m, 0, set_up, quarter, (1,))

        def body_of(side):
            ref = lower if side == 0 else upper

            def body(b, carry):
                windows = [
                    field[RES + m, slab, pl.ds(b, small + 2 * PAD), :]
                    - step_size * field[IMG + m, slab, pl.ds(b, small + 2 * PAD), :]
                    for slab in range(2)
                ]
                beside = (
                    ref[H_RES + m, pl.ds(b, small), :]
                    - step_size * ref[H_IMG + m, pl.ds(b, small), :]
                )
                term = 2.0 * across[2 * side, pl.ds(b, small), :] * beside
                outer = (term, None) if side == 0 else (None, term)
                centre, images = heat(windows, outer, b, small)
                norm, along = carry
                for slab in range(2):
                    v = centre[slab]
                    norm = norm + folded(v * v)
                    along = along + folded(v * (v - WIDTHS[m] * images[slab]))
                return norm, along

            return body

        nothing = jnp.zeros((8, nz), f32)
        carry = loop(quarter, small, body_of(0), (nothing, nothing), set_up)
        carry = loop(quarter, small, body_of(1), carry, set_down)
        sum_start(2 * m + 1, carry)
        return norm_now, step_size

    def factors(m, norm_now, step_size):
        norm_next, along = sum_wait(2 * m + 1)
        momentum = norm_next / norm_now
        step_next = norm_next / (along - momentum * norm_next / step_size)
        return step_size + step_next * (1.0 + momentum), step_size * step_next

    def finish(m, scalars):
        on_res, on_img = factors(m, *scalars)
        node = NODE + min(m, 2)

        def body(b, carry):
            at = pl.ds(PAD + b, tile)
            for slab in range(2):
                x = (
                    field[node, slab, at, :]
                    + on_res * field[RES + m, slab, at, :]
                    - on_img * field[IMG + m, slab, at, :]
                )
                result[m, slab, pl.ds(b, tile), :] = x
                if m < 2:
                    field[RES + m + 1, slab, at, :] = x + base[m, slab, pl.ds(b, tile), :]
            return carry

        loop(win, tile, body)

    def old_image(j):
        for c in range(chunks):
            halo_wait(H_NODE + j, c, c * chunk, chunk)

        def body(b, carry):
            _, images = plain_heat(NODE + j, H_NODE + j, b, tile)
            for slab in range(2):
                image[j, slab, pl.ds(b, tile), :] = images[slab]
            return carry

        loop(win, tile, body)

    pass_on(KAPPA)
    pass_on(NODE)
    for c in range(chunks):
        halo_wait(H_KAPPA, c, c * chunk, chunk)
    loop(win, tile, coefficients)
    pass_on(NODE + 1)
    old_image(0)
    pass_on(NODE + 2)
    old_image(1)
    for c in range(chunks):
        swap_wait(START, c)
    for c in range(chunks):
        halo_wait(H_NODE + 2, c, c * chunk, chunk)

    def residuals(b, carry):
        _, last = plain_heat(NODE + 2, H_NODE + 2, b, tile)
        at = pl.ds(PAD + b, tile)
        for slab in range(2):
            images = [image[0, slab, pl.ds(b, tile), :], image[1, slab, pl.ds(b, tile), :], last[slab]]
            begin = field[START, slab, at, :]
            parts = []
            for row in range(4):
                weights = COLLOC[2] if row == 3 else [sweep_weight(row, j) for j in range(3)]
                value = (STEP * weights[0]) * images[0]
                for j in range(1, 3):
                    value = value + (STEP * weights[j]) * images[j]
                parts.append(value - field[NODE + min(row, 2), slab, at, :])
            field[RES, slab, at, :] = begin + parts[0]
            base[0, slab, pl.ds(b, tile), :] = parts[1]
            base[1, slab, pl.ds(b, tile), :] = parts[2]
            field[RES + 3, slab, at, :] = begin + parts[3]
        return carry

    loop(win, tile, residuals)

    def give_back(m):
        later(
            start(
                remote(
                    result.at[m, other, pl.ds(own, half)], fine_out.at[0, m, 0, pl.ds(mine, half)],
                    out_s.at[m], out_r.at[m], t, partner,
                )
            )
        )
        keep = pltpu.make_async_copy(
            result.at[m, h, pl.ds(own, half)], fine_out.at[0, m, 0, pl.ds(mine, half)], keep_s.at[m]
        )
        keep.start()
        return keep

    theirs = pl.multiple_of(other * half, 8)

    @pl.when(jnp.logical_not(has_prev))
    def _():
        pltpu.make_async_copy(start_in.at[0, 0], staged, copy_s.at[0]).start()

    res_send(0)
    product(0)
    res_send(3)
    scalars = second(0)
    finish(0, scalars)
    res_send(1)
    keeps = [give_back(0)]
    product(3)
    product(1)
    scalars = second(1)
    scalars_coarse = second(3)
    finish(1, scalars)
    res_send(2)
    keeps.append(give_back(1))
    finish(3, scalars_coarse)

    def coarse_copies():
        return [
            remote(
                result.at[3, h, pl.ds(own, half)], coarse_out.at[0, 0, pl.ds(mine, half)],
                end_s.at[0], end_r.at[0], t + 1, s,
            ),
            remote(
                result.at[3, other, pl.ds(own, half)], coarse_out.at[0, 0, pl.ds(mine, half)],
                end_s.at[1], end_r.at[1], t + 1, partner,
            ),
        ]

    for copy in coarse_copies():
        start(copy, has_next)
        later(copy, has_next)

    @pl.when(jnp.logical_not(has_prev))
    def _():
        pltpu.make_async_copy(start_in.at[0, 0], staged, copy_s.at[0]).wait()
        first = pltpu.make_async_copy(staged, start_out.at[0, 0], copy_s.at[0])
        second_copy = pltpu.make_async_copy(staged, coarse_out.at[0, 0], copy_s.at[1])
        first.start()
        second_copy.start()
        first.wait()
        second_copy.wait()

    product(2)
    scalars = second(2)
    finish(2, scalars)

    pieces = 2
    piece = half // pieces
    for c in range(pieces):
        later(
            start(
                remote(
                    result.at[2, other, pl.ds(own + c * piece, piece)],
                    mail.at[pl.ds(c * piece, piece)],
                    out_s.at[2 + c], out_r.at[2 + c], t, partner,
                )
            )
        )
    for c in range(pieces):
        rows = pl.ds(mine + c * piece, piece)
        src = result.at[2, h, pl.ds(own + c * piece, piece)]
        copy = remote(src, start_out.at[0, 0, rows], end_s.at[2 + c], end_r.at[2 + c], t + 1, s)
        start(copy, has_next)
        later(copy, has_next)
        keep = pltpu.make_async_copy(src, fine_out.at[0, 2, 0, rows], keep_s.at[2 + c])
        keep.start()
        keeps.append(keep)
    for c in range(pieces):
        rows = pl.ds(theirs + c * piece, piece)
        src = mail.at[pl.ds(c * piece, piece)]
        remote(src, src, out_s.at[2 + c], out_r.at[2 + c], t, partner).wait_recv()
        copy = remote(
            src, start_out.at[0, 0, rows],
            end_s.at[2 + pieces + c], end_r.at[2 + pieces + c], t + 1, s,
        )
        start(copy, has_next)
        later(copy, has_next)
        keep = pltpu.make_async_copy(src, fine_out.at[0, 2, 0, rows], keep_s.at[2 + pieces + c])
        keep.start()
        keeps.append(keep)

    for m in range(2):
        dst = fine_out.at[0, m, 0, pl.ds(theirs, half)]
        remote(dst, dst, out_s.at[m], out_r.at[m], t, partner).wait_recv()

    @pl.when(has_prev)
    def _():
        for k in range(2):
            at = mine if k == 0 else theirs
            dst = coarse_out.at[0, 0, pl.ds(at, half)]
            remote(dst, dst, end_s.at[k], end_r.at[k], t - 1, s).wait_recv()
        for k in range(2):
            at = mine if k == 0 else theirs
            for c in range(pieces):
                dst = start_out.at[0, 0, pl.ds(at + c * piece, piece)]
                e = 2 + k * pieces + c
                remote(dst, dst, end_s.at[e], end_r.at[e], t - 1, s).wait_recv()

    for keep in keeps:
        keep.wait()
    for copy, cond in pending:
        if cond is None:
            copy.wait_send()
        else:
            pl.when(cond)(copy.wait_send)

    def drain(d, carry):
        for e in range(8):
            sum_copy(e, d).wait_send()
        return carry

    lax.fori_loop(1, slabs, drain, 0)


def solution(mesh):
    slices, slabs = mesh.shape["tm"], mesh.shape["space"]

    def on_device(start_value, old_nodes, diffusivity):
        ny, nz = start_value.shape[2:]
        half = ny // 2
        win = half + PAD
        chunks = win // tile_of(win, win // 3)
        vmem = lambda *shape: pltpu.VMEM(shape, jnp.float32)
        dma = lambda *shape: pltpu.SemaphoreType.DMA(shape)

        def body(*refs):
            kernel(slices, slabs, ny, nz, *refs)

        return pl.pallas_call(
            body,
            out_shape=(
                jax.ShapeDtypeStruct(old_nodes.shape, jnp.float32),
                jax.ShapeDtypeStruct(start_value.shape, jnp.float32),
                jax.ShapeDtypeStruct(start_value.shape, jnp.float32),
            ),
            in_specs=[pl.BlockSpec(memory_space=pl.ANY)] * 3,
            out_specs=(pl.BlockSpec(memory_space=pl.ANY),) * 3,
            scratch_shapes=[
                vmem(FIELDS, 2, win + 2 * PAD, nz),
                vmem(HALOS, win, nz),
                vmem(HALOS, win, nz),
                vmem(4, 2, win, nz),
                vmem(3, win, nz),
                vmem(2, 2, win, nz),
                vmem(2, 2, win, nz),
                vmem(4, 2, win, nz),
                vmem(ny, nz),
                vmem(half, nz),
                vmem(8, slabs, 2, 128),
                dma(5, chunks), dma(5, chunks), dma(5),
                dma(HALOS, 2, chunks), dma(HALOS, 2, chunks),
                dma(8, slabs), dma(8, slabs),
                dma(4), dma(4), dma(6), dma(6), dma(6), dma(2),
            ],
            compiler_params=pltpu.CompilerParams(
                collective_id=0, has_side_effects=True, vmem_limit_bytes=60 * 1024 * 1024
            ),
            name="pfasst",
        )(start_value, old_nodes, diffusivity)

    in_specs = (
        P("tm", "space", None, None),
        P("tm", None, "space", None, None),
        P("space", None, None),
    )
    out_specs = (
        P("tm", None, "space", None, None),
        P("tm", "space", None, None),
        P("tm", "space", None, None),
    )
    return jax.shard_map(
        on_device, mesh=mesh, in_specs=in_specs, out_specs=out_specs, check_vma=False
    )
```

time: 454 us -> 112 us (0.25)
  the two profiles are of different devices: /device:TPU:1 before, /device:TPU:0 now
where the time goes in v1:
time: 112 us
  Pallas kernels  107 us (96%)
  local copies, waits for them, and re-layouts  4.33 us (4%)
    pallas_call x1, Pallas kernels, on_device(): pl.pallas_call(body, out_shape=(jax.ShapeDtypeStruct(old_nodes.shape, jnp...  107 us
    unnamed x7, local copies, waits for them, and re-layouts  4.33 us

profile of v1, /device:TPU:0, one launch (start us, length us, event | category | flops | bytes accessed | tf_op | source)
XLA Modules:
  0.0 111.7 jit_solution(11635909837394415636)
XLA Ops:
  0.6 106.7 %pfasst.1 = (f32[1,3,1,512,256]{4,3,2,1,0:T(8,128)}, f32[1,1,512,256]{3,2,1,0:T(8,128)}, f32[1,1,512,256]{3,2,1,0:T(8,128)}) custom-call(f32[1,1,512,256]{3,2,1,0:T(8,128)} %refs_0_.1, f32[1,3,1,512,256]{4,3,2,1,0:T(8,128)} %refs_1_.1, f32[1,512,256]{2,1,0:T(8,128)} %refs_2_.1), custom_call_target="tpu_custom_call" | custom-call | tf_op jit(solution)/shard_map/pfasst/pallas_call | solution.py:627
  107.4 0.0 copy-start.1
  107.4 0.0 copy-start
  107.4 2.7 %copy.9 = f32[1,3,1,512,256]{4,3,2,1,0:T(8,128)} copy(f32[1,3,1,512,256]{4,3,2,1,0:T(8,128)} %get-tuple-element.6) | data formatting | bytes 3145728
  110.1 0.0 copy-done.1
  110.1 0.8 copy.10
  110.9 0.0 copy-done
  110.9 0.8 copy.11
Async XLA Ops:
  107.4 2.8 %copy-start.1 = (f32[1,1,512,256]{3,2,1,0:T(8,128)S(1)}, f32[1,1,512,256]{3,2,1,0:T(8,128)}, u32[]{:S(2)}) copy-start(f32[1,1,512,256]{3,2,1,0:T(8,128)} %get-tuple-element.7) | copy-start | bytes 1572868
  107.4 3.5 %copy-start = (f32[1,1,512,256]{3,2,1,0:T(8,128)S(1)}, f32[1,1,512,256]{3,2,1,0:T(8,128)}, u32[]{:S(2)}) copy-start(f32[1,1,512,256]{3,2,1,0:T(8,128)} %get-tuple-element.8) | copy-start | bytes 1572868

commit v2 on v1

--- a/solution.py
+++ b/solution.py
@@ -26,10 +26,10 @@
 MESH = pl.DeviceIdType.MESH
 PAD = 8
 
-KAPPA, NODE, START, RES, IMG = 0, 1, 4, 5, 9
-FIELDS = 13
-H_KAPPA, H_NODE, H_RES, H_IMG = 0, 1, 4, 8
-HALOS = 12
+KAPPA, NODE, START, RES, IMG, GAIN = 0, 1, 4, 5, 9, 13
+FIELDS = 15
+H_KAPPA, H_NODE, H_RES, H_IMG, H_GAIN = 0, 1, 4, 8, 12
+HALOS = 14
 
 
 def sweep_weight(row, column):
@@ -43,6 +43,13 @@
 
 
 WIDTHS = [STEP * node_width(0), STEP * node_width(1), STEP * node_width(2), STEP]
+
+
+def chunk_bounds(rows, tile):
+    tiles = rows // tile
+    parts = min(3, tiles)
+    cuts = [tile * (-(-tiles * c // parts)) for c in range(parts + 1)]
+    return [(cuts[c], cuts[c + 1] - cuts[c]) for c in range(parts)]
 
 
 def tile_of(rows, most):
@@ -57,7 +64,7 @@
     slices, slabs, ny, nz,
     start_in, nodes_in, kappa_in,
     fine_out, start_out, coarse_out,
-    field, lower, upper, faces, across, image, base, result, staged, mail, sums,
+    field, lower, upper, faces, across, result, staged, mail, sums,
     swap_s, swap_r, own_s, halo_s, halo_r, sum_s, sum_r, out_s, out_r, keep_s, end_s, end_r, copy_s,
 ):
     f32 = jnp.float32
@@ -150,25 +157,25 @@
         slabs - 1 + 2 * has_next.astype(jnp.int32) + 2 * has_prev.astype(jnp.int32),
     )
 
-    chunk = tile_of(win, win // 3)
-    chunks = win // chunk
+    tile = tile_of(win, 24)
+    bounds = chunk_bounds(win, tile)
+    chunks = len(bounds)
 
     def swap_copy(k, c):
+        lo, rows = bounds[c]
         return remote(
-            sources[k].at[pl.ds(partner_row + c * chunk, chunk)],
-            field.at[k, h, pl.ds(PAD + c * chunk, chunk)],
+            sources[k].at[pl.ds(partner_row + lo, rows)],
+            field.at[k, h, pl.ds(PAD + lo, rows)],
             swap_s.at[k, c], swap_r.at[k, c], t, partner,
         )
 
     def swap_wait(k, c):
-        remote(
-            field.at[k, other, pl.ds(PAD + c * chunk, chunk)],
-            field.at[k, other, pl.ds(PAD + c * chunk, chunk)],
-            swap_s.at[k, c], swap_r.at[k, c], t, partner,
-        ).wait_recv()
-
-    for k in range(5):
-        for c in range(chunks):
+        lo, rows = bounds[c]
+        dst = field.at[k, other, pl.ds(PAD + lo, rows)]
+        remote(dst, dst, swap_s.at[k, c], swap_r.at[k, c], t, partner).wait_recv()
+
+    for c in range(chunks):
+        for k in range(5):
             later(start(swap_copy(k, c)))
 
     def down(f, k, c, lo, rows):
@@ -186,22 +193,17 @@
     def first_hop(k, c, which):
         @pl.when(jnp.logical_and(which == 0, has_lower))
         def _():
-            down(k, k, c, c * chunk, chunk).start()
+            down(k, k, c, *bounds[c]).start()
 
         @pl.when(jnp.logical_and(which == 1, has_upper))
         def _():
-            up(k, k, c, c * chunk, chunk).start()
-
-    for k in range(4):
-        loads[k].wait()
-        for c in range(chunks):
+            up(k, k, c, *bounds[c]).start()
+
+    for copy in loads:
+        copy.wait()
+    for c in range(chunks):
+        for k in range(4):
             first_hop(k, c, h)
-    loads[4].wait()
-
-    def pass_on(k):
-        for c in range(chunks):
-            swap_wait(k, c)
-            first_hop(k, c, other)
 
     def halo_wait(k, c, lo, rows, sides=(0, 1)):
         if 0 in sides:
@@ -228,9 +230,8 @@
 
     for k in range(4):
         for c in range(chunks):
-            halo_sent(k, k, c, c * chunk, chunk)
-
-    tile = tile_of(win, 24)
+            halo_sent(k, k, c, *bounds[c])
+
     lane = lax.broadcasted_iota(jnp.int32, (tile, nz), 1)
 
     def loop(rows, size, body, init=0, offset=0):
@@ -324,27 +325,34 @@
         total = jnp.sum(total, axis=1, keepdims=True)
         return total[0:1, :], total[1:2, :]
 
-    def res_send(m):
-        start(down(RES + m, H_RES + m, 0, 0, win), has_lower)
-        start(up(RES + m, H_RES + m, 0, 0, win), has_upper)
-        halo_sent(RES + m, H_RES + m, 0, 0, win)
+    def halo_send(f, k, c, lo, rows):
+        start(down(f, k, c, lo, rows), has_lower)
+        start(up(f, k, c, lo, rows), has_upper)
+        halo_sent(f, k, c, lo, rows)
 
     quarter = half // 2
     set_up = own
     set_down = pl.multiple_of(own + quarter, 8)
-
-    def img_send(m):
+    pieces_of = (
+        ((quarter, quarter + PAD), (0, quarter + PAD)),
+        ((0, quarter), (quarter + PAD, quarter)),
+    )
+
+    def img_send(m, piece):
+        (lo_d, rows_d), (lo_u, rows_u) = pieces_of[piece]
         copies = (
-            (down(IMG + m, H_IMG + m, 0, set_down, quarter), has_lower),
-            (up(IMG + m, H_IMG + m, 0, set_up, quarter), has_upper),
+            (down(IMG + m, H_IMG + m, piece, lo_d, rows_d), has_lower),
+            (up(IMG + m, H_IMG + m, piece, lo_u, rows_u), has_upper),
         )
         for copy, cond in copies:
             start(copy, cond)
             later(copy, cond)
 
+    def img_wait(m, piece):
+        halo_wait(H_IMG + m, piece, *pieces_of[piece][0], (0,))
+        halo_wait(H_IMG + m, piece, *pieces_of[piece][1], (1,))
+
     def product(m):
-        halo_wait(H_RES + m, 0, 0, win)
-
         def body(b, carry):
             centre, images = plain_heat(RES + m, H_RES + m, b, tile)
             row = lax.broadcasted_iota(jnp.int32, (tile, nz), 0) + b
@@ -361,16 +369,15 @@
 
         nothing = jnp.zeros((8, nz), f32)
         norm, along = loop(win, tile, body, (nothing, nothing))
-        img_send(m)
         sum_start(2 * m, (norm, along))
+        img_send(m, 0)
 
     small = tile_of(quarter, 32)
 
     def second(m):
         norm_now, along = sum_wait(2 * m)
         step_size = norm_now / along
-        halo_wait(H_IMG + m, 0, set_down, quarter, (0,))
-        halo_wait(H_IMG + m, 0, set_up, quarter, (1,))
+        img_wait(m, 0)
 
         def body_of(side):
             ref = lower if side == 0 else upper
@@ -409,71 +416,104 @@
         step_next = norm_next / (along - momentum * norm_next / step_size)
         return step_size + step_next * (1.0 + momentum), step_size * step_next
 
-    def finish(m, scalars):
-        on_res, on_img = factors(m, *scalars)
-        node = NODE + min(m, 2)
+    def advance(m, scalars):
+        on_res, on_img = scalars
+        for c in range(chunks):
+            halo_wait(H_GAIN + m, c, *spans[c])
+        img_wait(m, 1)
 
         def body(b, carry):
             at = pl.ds(PAD + b, tile)
+            rows = pl.ds(b, tile)
             for slab in range(2):
-                x = (
+                field[RES + m + 1, slab, at, :] = (
+                    field[GAIN + m, slab, at, :]
+                    + on_res * field[RES + m, slab, at, :]
+                    - on_img * field[IMG + m, slab, at, :]
+                )
+            for ref in (lower, upper):
+                ref[H_RES + m + 1, rows, :] = (
+                    ref[H_GAIN + m, rows, :]
+                    + on_res * ref[H_RES + m, rows, :]
+                    - on_img * ref[H_IMG + m, rows, :]
+                )
+            return carry
+
+        loop(win, tile, body)
+
+    def coarse_residual():
+        def body(b, carry):
+            at = pl.ds(PAD + b, tile)
+            rows = pl.ds(b, tile)
+            for slab in range(2):
+                field[RES + 3, slab, at, :] = (
+                    field[RES, slab, at, :] + field[GAIN, slab, at, :] + field[GAIN + 1, slab, at, :]
+                )
+            for ref in (lower, upper):
+                ref[H_RES + 3, rows, :] = (
+                    ref[H_RES, rows, :] + ref[H_GAIN, rows, :] + ref[H_GAIN + 1, rows, :]
+                )
+            return carry
+
+        loop(win, tile, body)
+
+    def finish(m, scalars):
+        on_res, on_img = scalars
+        node = NODE + min(m, 2)
+
+        def body(b, carry):
+            for slab in range(2):
+                at = pl.ds(PAD + b, small)
+                result[m, slab, pl.ds(b, small), :] = (
                     field[node, slab, at, :]
                     + on_res * field[RES + m, slab, at, :]
                     - on_img * field[IMG + m, slab, at, :]
                 )
-                result[m, slab, pl.ds(b, tile), :] = x
-                if m < 2:
-                    field[RES + m + 1, slab, at, :] = x + base[m, slab, pl.ds(b, tile), :]
             return carry
 
-        loop(win, tile, body)
-
-    def old_image(j):
-        for c in range(chunks):
-            halo_wait(H_NODE + j, c, c * chunk, chunk)
-
-        def body(b, carry):
-            _, images = plain_heat(NODE + j, H_NODE + j, b, tile)
-            for slab in range(2):
-                image[j, slab, pl.ds(b, tile), :] = images[slab]
-            return carry
-
-        loop(win, tile, body)
-
-    pass_on(KAPPA)
-    pass_on(NODE)
-    for c in range(chunks):
-        halo_wait(H_KAPPA, c, c * chunk, chunk)
-    loop(win, tile, coefficients)
-    pass_on(NODE + 1)
-    old_image(0)
-    pass_on(NODE + 2)
-    old_image(1)
-    for c in range(chunks):
-        swap_wait(START, c)
-    for c in range(chunks):
-        halo_wait(H_NODE + 2, c, c * chunk, chunk)
+        loop(half, small, body, 0, own)
 
     def residuals(b, carry):
-        _, last = plain_heat(NODE + 2, H_NODE + 2, b, tile)
+        images = [plain_heat(NODE + j, H_NODE + j, b, tile)[1] for j in range(3)]
         at = pl.ds(PAD + b, tile)
         for slab in range(2):
-            images = [image[0, slab, pl.ds(b, tile), :], image[1, slab, pl.ds(b, tile), :], last[slab]]
-            begin = field[START, slab, at, :]
-            parts = []
-            for row in range(4):
-                weights = COLLOC[2] if row == 3 else [sweep_weight(row, j) for j in range(3)]
-                value = (STEP * weights[0]) * images[0]
-                for j in range(1, 3):
-                    value = value + (STEP * weights[j]) * images[j]
-                parts.append(value - field[NODE + min(row, 2), slab, at, :])
-            field[RES, slab, at, :] = begin + parts[0]
-            base[0, slab, pl.ds(b, tile), :] = parts[1]
-            base[1, slab, pl.ds(b, tile), :] = parts[2]
-            field[RES + 3, slab, at, :] = begin + parts[3]
+            nodes = [field[NODE + j, slab, at, :] for j in range(3)]
+            ahead = [field[START, slab, at, :]] + nodes
+            for row, f in enumerate((RES, GAIN, GAIN + 1)):
+                value = ahead[row] - nodes[row]
+                for j in range(3):
+                    value = value + (STEP * sweep_weight(row, j)) * images[j][slab]
+                field[f, slab, at, :] = value
         return carry
 
-    loop(win, tile, residuals)
+    spans = []
+    for c, (lo, rows) in enumerate(bounds):
+        begin = lo - tile if c else 0
+        end = lo + rows - (tile if c < chunks - 1 else 0)
+        spans.append((begin, end - begin))
+
+    def begin_rows(c):
+        for k in range(4):
+            halo_wait(k, c, *bounds[c])
+        lo, rows = spans[c]
+        loop(rows, tile, coefficients, 0, lo)
+        loop(rows, tile, residuals, 0, lo)
+        halo_send(RES, H_RES, c, lo, rows)
+        if c == 0:
+            halo_send(GAIN, H_GAIN, c, lo, rows)
+
+    order = [(k, c) for c in range(chunks) for k in range(5)]
+    ready = {}
+    for c in range(chunks):
+        ready[min(5 * c + 6, len(order) - 1)] = c
+    for n, (k, c) in enumerate(order):
+        swap_wait(k, c)
+        if k < 4:
+            first_hop(k, c, other)
+        if n in ready:
+            begin_rows(ready[n])
+    for c in range(1, chunks - 1):
+        halo_send(GAIN, H_GAIN, c, *spans[c])
 
     def give_back(m):
         later(
@@ -496,21 +536,65 @@
     def _():
         pltpu.make_async_copy(start_in.at[0, 0], staged, copy_s.at[0]).start()
 
-    res_send(0)
+    for c in range(chunks):
+        halo_wait(H_RES, c, *spans[c])
     product(0)
-    res_send(3)
+    halo_send(GAIN, H_GAIN, chunks - 1, *spans[chunks - 1])
     scalars = second(0)
-    finish(0, scalars)
-    res_send(1)
+    img_send(0, 1)
+    halo_send(GAIN + 1, H_GAIN + 1, 0, *spans[0])
+    update = factors(0, *scalars)
+    advance(0, update)
+    product(1)
+    for c in range(1, chunks - 1):
+        halo_send(GAIN + 1, H_GAIN + 1, c, *spans[c])
+    finish(0, update)
     keeps = [give_back(0)]
+    @pl.when(jnp.logical_not(has_prev))
+    def _():
+        pltpu.make_async_copy(start_in.at[0, 0], staged, copy_s.at[0]).wait()
+        first = pltpu.make_async_copy(staged, start_out.at[0, 0], copy_s.at[0])
+        second_copy = pltpu.make_async_copy(staged, coarse_out.at[0, 0], copy_s.at[1])
+        first.start()
+        second_copy.start()
+        first.wait()
+        second_copy.wait()
+
+    scalars = second(1)
+    img_send(1, 1)
+    halo_send(GAIN + 1, H_GAIN + 1, chunks - 1, *spans[chunks - 1])
+    update = factors(1, *scalars)
+    advance(1, update)
+    product(2)
+    coarse_residual()
     product(3)
-    product(1)
-    scalars = second(1)
+    scalars = second(2)
+    finish(1, update)
+    keeps.append(give_back(1))
     scalars_coarse = second(3)
-    finish(1, scalars)
-    res_send(2)
-    keeps.append(give_back(1))
-    finish(3, scalars_coarse)
+    finish(2, factors(2, *scalars))
+    pieces = 2
+    piece = half // pieces
+    for c in range(pieces):
+        later(
+            start(
+                remote(
+                    result.at[2, other, pl.ds(own + c * piece, piece)],
+                    mail.at[pl.ds(c * piece, piece)],
+                    out_s.at[2 + c], out_r.at[2 + c], t, partner,
+                )
+            )
+        )
+    for c in range(pieces):
+        rows = pl.ds(mine + c * piece, piece)
+        src = result.at[2, h, pl.ds(own + c * piece, piece)]
+        copy = remote(src, start_out.at[0, 0, rows], end_s.at[2 + c], end_r.at[2 + c], t + 1, s)
+        start(copy, has_next)
+        later(copy, has_next)
+        keep = pltpu.make_async_copy(src, fine_out.at[0, 2, 0, rows], keep_s.at[2 + c])
+        keep.start()
+        keeps.append(keep)
+    finish(3, factors(3, *scalars_coarse))
 
     def coarse_copies():
         return [
@@ -528,41 +612,6 @@
         start(copy, has_next)
         later(copy, has_next)
 
-    @pl.when(jnp.logical_not(has_prev))
-    def _():
-        pltpu.make_async_copy(start_in.at[0, 0], staged, copy_s.at[0]).wait()
-        first = pltpu.make_async_copy(staged, start_out.at[0, 0], copy_s.at[0])
-        second_copy = pltpu.make_async_copy(staged, coarse_out.at[0, 0], copy_s.at[1])
-        first.start()
-        second_copy.start()
-        first.wait()
-        second_copy.wait()
-
-    product(2)
-    scalars = second(2)
-    finish(2, scalars)
-
-    pieces = 2
-    piece = half // pieces
-    for c in range(pieces):
-        later(
-            start(
-                remote(
-                    result.at[2, other, pl.ds(own + c * piece, piece)],
-                    mail.at[pl.ds(c * piece, piece)],
-                    out_s.at[2 + c], out_r.at[2 + c], t, partner,
-                )
-            )
-        )
-    for c in range(pieces):
-        rows = pl.ds(mine + c * piece, piece)
-        src = result.at[2, h, pl.ds(own + c * piece, piece)]
-        copy = remote(src, start_out.at[0, 0, rows], end_s.at[2 + c], end_r.at[2 + c], t + 1, s)
-        start(copy, has_next)
-        later(copy, has_next)
-        keep = pltpu.make_async_copy(src, fine_out.at[0, 2, 0, rows], keep_s.at[2 + c])
-        keep.start()
-        keeps.append(keep)
     for c in range(pieces):
         rows = pl.ds(theirs + c * piece, piece)
         src = mail.at[pl.ds(c * piece, piece)]
@@ -617,7 +666,7 @@
         ny, nz = start_value.shape[2:]
         half = ny // 2
         win = half + PAD
-        chunks = win // tile_of(win, win // 3)
+        chunks = len(chunk_bounds(win, tile_of(win, 24)))
         vmem = lambda *shape: pltpu.VMEM(shape, jnp.float32)
         dma = lambda *shape: pltpu.SemaphoreType.DMA(shape)
 
@@ -639,8 +688,6 @@
                 vmem(HALOS, win, nz),
                 vmem(4, 2, win, nz),
                 vmem(3, win, nz),
-                vmem(2, 2, win, nz),
-                vmem(2, 2, win, nz),
                 vmem(4, 2, win, nz),
                 vmem(ny, nz),
                 vmem(half, nz),

time: 112 us -> 104 us (0.929)
  the two profiles are of different devices: /device:TPU:0 before, /device:TPU:3 now
where the time goes in v2:
time: 104 us; the launch traced here: 103 us
  Pallas kernels  98.3 us (95%)
  local copies, waits for them, and re-layouts  4.33 us (4%)
    pallas_call x1, Pallas kernels, on_device(): pl.pallas_call(body, out_shape=(jax.ShapeDtypeStruct(old_nodes.shape, jnp...  98.3 us
    unnamed x7, local copies, waits for them, and re-layouts  4.33 us

profile of v2, /device:TPU:3, one launch (start us, length us, event | category | flops | bytes accessed | tf_op | source)
XLA Modules:
  0.0 103.3 jit_solution(16178730544594631013)
XLA Ops:
  0.6 98.3 %pfasst.1 = (f32[1,3,1,512,256]{4,3,2,1,0:T(8,128)}, f32[1,1,512,256]{3,2,1,0:T(8,128)}, f32[1,1,512,256]{3,2,1,0:T(8,128)}) custom-call(f32[1,1,512,256]{3,2,1,0:T(8,128)} %refs_0_.1, f32[1,3,1,512,256]{4,3,2,1,0:T(8,128)} %refs_1_.1, f32[1,512,256]{2,1,0:T(8,128)} %refs_2_.1), custom_call_target="tpu_custom_call" | custom-call | tf_op jit(solution)/shard_map/pfasst/pallas_call | solution.py:676
  99.0 0.0 copy-start.1
  99.0 0.0 copy-start
  99.0 2.7 %copy.9 = f32[1,3,1,512,256]{4,3,2,1,0:T(8,128)} copy(f32[1,3,1,512,256]{4,3,2,1,0:T(8,128)} %get-tuple-element.6) | data formatting | bytes 3145728
  101.7 0.0 copy-done.1
  101.7 0.8 copy.10
  102.5 0.0 copy-done
  102.5 0.8 copy.11
Async XLA Ops:
  99.0 2.8 %copy-start.1 = (f32[1,1,512,256]{3,2,1,0:T(8,128)S(1)}, f32[1,1,512,256]{3,2,1,0:T(8,128)}, u32[]{:S(2)}) copy-start(f32[1,1,512,256]{3,2,1,0:T(8,128)} %get-tuple-element.7) | copy-start | bytes 1572868
  99.0 3.5 %copy-start = (f32[1,1,512,256]{3,2,1,0:T(8,128)S(1)}, f32[1,1,512,256]{3,2,1,0:T(8,128)}, u32[]{:S(2)}) copy-start(f32[1,1,512,256]{3,2,1,0:T(8,128)} %get-tuple-element.8) | copy-start | bytes 1572868

commit v3 on v2

--- a/solution.py
+++ b/solution.py
@@ -47,7 +47,7 @@
 
 def chunk_bounds(rows, tile):
     tiles = rows // tile
-    parts = min(3, tiles)
+    parts = min(5, tiles)
     cuts = [tile * (-(-tiles * c // parts)) for c in range(parts + 1)]
     return [(cuts[c], cuts[c + 1] - cuts[c]) for c in range(parts)]
 

time: 104 us -> 102 us (0.981)
  Pallas kernels: 98.3 us -> 96.6 us
    pallas_call x1, Pallas kernels: 98.3 us -> 96.6 us  [on_device(): pl.pallas_call(body, out_shape=(jax.ShapeDtypeStruct(old_nodes.shape, jnp...]
where the time goes in v3:
time: 102 us
  Pallas kernels  96.6 us (95%)
  local copies, waits for them, and re-layouts  4.33 us (4%)
    pallas_call x1, Pallas kernels, on_device(): pl.pallas_call(body, out_shape=(jax.ShapeDtypeStruct(old_nodes.shape, jnp...  96.6 us
    unnamed x7, local copies, waits for them, and re-layouts  4.33 us

profile of v3, /device:TPU:3, one launch (start us, length us, event | category | flops | bytes accessed | tf_op | source)
XLA Modules:
  0.0 101.6 jit_solution(17917298351670181200)
XLA Ops:
  0.6 96.6 %pfasst.1 = (f32[1,3,1,512,256]{4,3,2,1,0:T(8,128)}, f32[1,1,512,256]{3,2,1,0:T(8,128)}, f32[1,1,512,256]{3,2,1,0:T(8,128)}) custom-call(f32[1,1,512,256]{3,2,1,0:T(8,128)} %refs_0_.1, f32[1,3,1,512,256]{4,3,2,1,0:T(8,128)} %refs_1_.1, f32[1,512,256]{2,1,0:T(8,128)} %refs_2_.1), custom_call_target="tpu_custom_call" | custom-call | tf_op jit(solution)/shard_map/pfasst/pallas_call | solution.py:676
  97.2 0.0 copy-start.1
  97.3 0.0 copy-start
  97.3 2.7 %copy.9 = f32[1,3,1,512,256]{4,3,2,1,0:T(8,128)} copy(f32[1,3,1,512,256]{4,3,2,1,0:T(8,128)} %get-tuple-element.6) | data formatting | bytes 3145728
  100.0 0.0 copy-done.1
  100.0 0.8 copy.10
  100.8 0.0 copy-done
  100.8 0.8 copy.11
Async XLA Ops:
  97.2 2.8 %copy-start.1 = (f32[1,1,512,256]{3,2,1,0:T(8,128)S(1)}, f32[1,1,512,256]{3,2,1,0:T(8,128)}, u32[]{:S(2)}) copy-start(f32[1,1,512,256]{3,2,1,0:T(8,128)} %get-tuple-element.7) | copy-start | bytes 1572868
  97.3 3.5 %copy-start = (f32[1,1,512,256]{3,2,1,0:T(8,128)S(1)}, f32[1,1,512,256]{3,2,1,0:T(8,128)}, u32[]{:S(2)}) copy-start(f32[1,1,512,256]{3,2,1,0:T(8,128)} %get-tuple-element.8) | copy-start | bytes 1572868

commit v4 on v3

--- a/solution.py
+++ b/solution.py
@@ -573,7 +573,7 @@
     keeps.append(give_back(1))
     scalars_coarse = second(3)
     finish(2, factors(2, *scalars))
-    pieces = 2
+    pieces = 4
     piece = half // pieces
     for c in range(pieces):
         later(
@@ -695,7 +695,7 @@
                 dma(5, chunks), dma(5, chunks), dma(5),
                 dma(HALOS, 2, chunks), dma(HALOS, 2, chunks),
                 dma(8, slabs), dma(8, slabs),
-                dma(4), dma(4), dma(6), dma(6), dma(6), dma(2),
+                dma(6), dma(6), dma(10), dma(10), dma(10), dma(2),
             ],
             compiler_params=pltpu.CompilerParams(
                 collective_id=0, has_side_effects=True, vmem_limit_bytes=60 * 1024 * 1024

time: 102 us -> 102 us (level)
  no operation moved by 1% of the time
where the time goes in v4:
time: 102 us
  Pallas kernels  96.8 us (95%)
  local copies, waits for them, and re-layouts  4.33 us (4%)
    pallas_call x1, Pallas kernels, on_device(): pl.pallas_call(body, out_shape=(jax.ShapeDtypeStruct(old_nodes.shape, jnp...  96.8 us
    unnamed x7, local copies, waits for them, and re-layouts  4.33 us

profile of v4, /device:TPU:3, one launch (start us, length us, event | category | flops | bytes accessed | tf_op | source)
XLA Modules:
  0.0 101.8 jit_solution(14922154268852785766)
XLA Ops:
  0.6 96.8 %pfasst.1 = (f32[1,3,1,512,256]{4,3,2,1,0:T(8,128)}, f32[1,1,512,256]{3,2,1,0:T(8,128)}, f32[1,1,512,256]{3,2,1,0:T(8,128)}) custom-call(f32[1,1,512,256]{3,2,1,0:T(8,128)} %refs_0_.1, f32[1,3,1,512,256]{4,3,2,1,0:T(8,128)} %refs_1_.1, f32[1,512,256]{2,1,0:T(8,128)} %refs_2_.1), custom_call_target="tpu_custom_call" | custom-call | tf_op jit(solution)/shard_map/pfasst/pallas_call | solution.py:676
  97.4 0.0 copy-start.1
  97.4 0.0 copy-start
  97.4 2.7 %copy.9 = f32[1,3,1,512,256]{4,3,2,1,0:T(8,128)} copy(f32[1,3,1,512,256]{4,3,2,1,0:T(8,128)} %get-tuple-element.6) | data formatting | bytes 3145728
  100.2 0.0 copy-done.1
  100.2 0.8 copy.10
  101.0 0.0 copy-done
  101.0 0.8 copy.11
Async XLA Ops:
  97.4 2.8 %copy-start.1 = (f32[1,1,512,256]{3,2,1,0:T(8,128)S(1)}, f32[1,1,512,256]{3,2,1,0:T(8,128)}, u32[]{:S(2)}) copy-start(f32[1,1,512,256]{3,2,1,0:T(8,128)} %get-tuple-element.7) | copy-start | bytes 1572868
  97.4 3.5 %copy-start = (f32[1,1,512,256]{3,2,1,0:T(8,128)S(1)}, f32[1,1,512,256]{3,2,1,0:T(8,128)}, u32[]{:S(2)}) copy-start(f32[1,1,512,256]{3,2,1,0:T(8,128)} %get-tuple-element.8) | copy-start | bytes 1572868
